TPU v7x, 32 devices: a whole 2x2x4 slice. The times are simulated.
32 devices in a mesh: pool: 2 (over x), dp: 4 (over z), mp: 4 (over y, core).
Axes of the slice: x: 2, y: 2, z: 4, core: 2. Of those that a mesh axis runs over, the one named last changes fastest.
Arguments:
- states: bfloat16 [2, 4, 512, 8192], P('pool', 'dp', 'mp'), may hold values from -8 to 8
- lengths: int32 [2, 4], P(None, 'dp'), may hold values from 128 to 512
- gain: bfloat16 [2, 8192], replicated, may hold values from 0.099609375 to 1.8984375
- w_query: bfloat16 [2, 8192, 4096], P('pool', ('dp', 'mp')), may hold values from -0.088388348 to 0.088388348
- w_keyval: bfloat16 [2, 8192, 1024], P('pool', ('dp', 'mp')), may hold values from -0.088388348 to 0.088388348
Outputs:
- attended: bfloat16 [2, 4, 512, 4096], P('pool', 'dp', None, 'mp')
Inputs may be any that keep to these rules, and one draw needn't show every extreme that they name: `lengths`: live positions of each rollout; positions from it on are padding.
All inputs are finite; a program needn't handle non-finite values.
Results may differ from a plain program's by a relative error of at most 0.011.
Values may be sent and summed in bfloat16 or wider, within the bound.
No kernel may reach another device: no remote copies, remote signals or barrier semaphores. Data moves between devices by JAX's collectives and lax.ppermute only.
A program may use at most 128 MiB of HBM per device.

v0:
```python
import math
import jax
import jax.numpy as jnp
from jax import lax
from jax.sharding import PartitionSpec as P

HD = 128
QH = 32
KVH = 4


def partner(value, axis, distance):
    return lax.ppermute(value, axis, [(i, i ^ 1 << distance) for i in range(lax.axis_size(axis))])


def normalize(rows, gain_row):
    values = rows.astype(jnp.float32)
    meansq = jnp.mean(values * values, axis=-1, keepdims=True)
    return (values * lax.rsqrt(meansq + 1e-05) * gain_row.astype(jnp.float32)).astype(jnp.bfloat16)


def attend(query, keyval, length):
    seqlen = query.shape[0]
    local_heads = keyval.shape[1] // (2 * HD)
    groups = QH // KVH
    block = min(seqlen, 512)
    paired = keyval.reshape(seqlen, local_heads, 2 * HD)
    keys = paired[:, :, :HD]
    values = paired[:, :, HD:]
    places = jnp.arange(seqlen, dtype=jnp.int32)

    def one_block(index):
        start = index * block
        rows = query.reshape(block, local_heads, groups, HD)
        scores = jnp.einsum(
            "tkgd,skd->kgts", rows, keys, preferred_element_type=jnp.float32
        ) / math.sqrt(HD)
        qplaces = start + jnp.arange(block, dtype=jnp.int32)
        allowed = (places[None, :] <= qplaces[:, None]) & (places[None, :] < length)
        scores = jnp.where(allowed, scores, jnp.float32(-1e30))
        peak = jnp.max(scores, axis=-1, keepdims=True)
        expo = jnp.exp(scores - peak)
        probs = (expo / jnp.sum(expo, axis=-1, keepdims=True)).astype(jnp.bfloat16)
        result = jnp.einsum("kgts,skd->tkgd", probs, values, preferred_element_type=jnp.float32)
        result = result * (qplaces < length).astype(jnp.float32)[:, None, None, None]
        return result.reshape(block, local_heads * groups * HD).astype(jnp.bfloat16)

    blocks = lax.map(one_block, jnp.arange(seqlen // block, dtype=jnp.int32))
    return blocks.reshape(seqlen, local_heads * groups * HD)


def on_device(states, lengths, gain, w_query, w_keyval):
    own = lax.axis_index("pool")
    other = 1 - own
    normed = normalize(states, lax.dynamic_index_in_dim(gain, own, 0, keepdims=False))
    local_rows = lax.all_gather(normed, "mp", axis=2, tiled=True)
    whole = partner(local_rows, "pool", 0)
    rollouts = whole.shape[1]
    seqlen = whole.shape[2]
    tokens = whole[0].reshape(rollouts * seqlen, whole.shape[3])
    rows_query, rows_keyval = partner((w_query, w_keyval), "pool", 0)
    query_cols, keyval_cols = (
        lax.all_to_all(rows_query, "mp", split_axis=2, concat_axis=1, tiled=True),
        lax.all_to_all(rows_keyval, "mp", split_axis=2, concat_axis=1, tiled=True),
    )
    width_query = query_cols.shape[2]
    width_keyval = keyval_cols.shape[2]
    full_query, full_keyval = (
        lax.all_gather(query_cols, "dp", axis=1, tiled=True),
        lax.all_gather(keyval_cols, "dp", axis=1, tiled=True),
    )
    query = jnp.dot(tokens, full_query[0], preferred_element_type=jnp.float32)
    keyval = jnp.dot(tokens, full_keyval[0], preferred_element_type=jnp.float32)
    query = query.astype(jnp.bfloat16).reshape(rollouts, seqlen, width_query)
    keyval = keyval.astype(jnp.bfloat16).reshape(rollouts, seqlen, width_keyval)
    live = lax.dynamic_index_in_dim(lengths, other, 0, keepdims=False)
    attended = jax.vmap(attend)(query, keyval, live)
    return attended[None]


def solution(mesh):
    in_specs = (
        P("pool", "dp", "mp", None),
        P(None, "dp"),
        P(),
        P("pool", ("dp", "mp"), None),
        P("pool", ("dp", "mp"), None),
    )
    out_specs = P("pool", "dp", None, "mp")
    return jax.shard_map(
        on_device, mesh=mesh, in_specs=in_specs, out_specs=out_specs, check_vma=False
    )
```

profile of v0, /device:TPU:0, one launch (start us, length us, event | category | flops | bytes accessed | tf_op | source)
XLA Modules:
  0.0 573.3 jit_solution(5611344158581876059)
XLA Ops:
  6.5 0.0 copy-start
  6.5 0.0 all-gather.4.cloned.1.call-start
  6.5 2.2 fusion.7
  8.7 0.8 dynamic-slice_convert_fusion
  9.5 3.5 fusion.9
  13.1 0.0 all-gather.4.cloned.1.call-update
  13.1 0.0 all-gather.6.cloned.1.call-start
  13.1 0.0 copy-done.2
  13.2 3.0 collective-permute-start.1
  16.2 0.1 collective-permute-start.2
  16.3 23.9 %collective-permute-done.1 = bf16[1,512,1024]{2,1,0:T(8,128)(2,1)S(1)} collective-permute-done((bf16[1,512,1024]{2,1,0:T(8,128)(2,1)S(1)}, bf16[1,512,1024]{2,1,0:T(8,128)(2,1)S(1)}, u32[]{:S(2)}, u32[]{:S(2)}) %collective-permute-start.1) | collective-permute-done | bytes 1048608 | tf_op jit(solution)/shard_map/ppermute | solution.py:13
  40.2 1.8 copy.30
  42.0 0.6 broadcast.68
  42.6 7.3 %reduce.4 = bf16[1024,512]{1,0:T(8,128)(2,1)S(1)} reduce(bf16[1024,1,512]{2,1,0:T(2,128)(2,1)S(1)} %bitcast.94, bf16[]{:T(256)} %broadcast.68), dimensions={1}, to_apply=%bitcast.83.reduce_sub_computation | reduce | bytes 2097154
  49.9 0.8 reshape.124
  50.7 29.2 %all_to_all.36 = bf16[4,2,65536]{2,1,0:T(2,128)(2,1)S(1)} all-to-all(bf16[4,2,65536]{2,1,0:T(2,128)(2,1)S(1)} %reshape.124), channel_id=1, replica_groups=mesh['pool'=2,'dp'=4,'mp'=4] {'mp'}, dimensions={0} | all-to-all | bytes 2097152 | tf_op jit(solution)/shard_map/all_to_all | solution.py:64
  79.9 1.0 reshape.125
  80.9 0.3 copy.41
  81.2 1.3 copy.31
  82.5 0.0 all-gather.6.cloned.1.call-update
  82.5 0.2 all-gather.8.cloned.1.call-start
  82.7 46.6 %collective-permute-done.2 = bf16[1,512,4096]{2,1,0:T(8,128)(2,1)} collective-permute-done((bf16[1,512,4096]{2,1,0:T(8,128)(2,1)}, bf16[1,512,4096]{2,1,0:T(8,128)(2,1)}, u32[]{:S(2)}, u32[]{:S(2)}) %collective-permute-start.2) | collective-permute-done | bytes 4194336 | tf_op jit(solution)/shard_map/ppermute | solution.py:13
  129.3 18.9 %copy.32 = bf16[1,512,4096]{1,0,2:T(2,128)(2,1)} copy(bf16[1,512,4096]{2,1,0:T(8,128)(2,1)} %collective-permute-done.2) | data formatting | bytes 8388608 | tf_op jit(solution)/shard_map/ppermute | solution.py:13
  148.2 28.5 %reduce.3 = bf16[4096,512]{1,0:T(8,128)(2,1)} reduce(bf16[4096,1,512]{2,1,0:T(2,128)(2,1)} %bitcast.89, bf16[]{:T(256)} %broadcast.68), dimensions={1}, to_apply=%bitcast.81.reduce_sub_computation | reduce | bytes 8388610
  176.7 6.2 %reshape.122 = bf16[4,2,262144]{2,1,0:T(2,128)(2,1)} reshape(bf16[4096,512]{1,0:T(8,128)(2,1)} %reduce.3) | data formatting | bytes 8388608
  182.9 53.8 %all_to_all.37 = bf16[4,2,262144]{2,1,0:T(2,128)(2,1)} all-to-all(bf16[4,2,262144]{2,1,0:T(2,128)(2,1)} %reshape.122), channel_id=1, replica_groups=mesh['pool'=2,'dp'=4,'mp'=4] {'mp'}, dimensions={0} | all-to-all | bytes 8388608 | tf_op jit(solution)/shard_map/all_to_all | solution.py:63
  236.8 7.4 %reshape.123 = bf16[4096,1,512]{2,1,0:T(2,128)(2,1)} reshape(bf16[4,2,262144]{2,1,0:T(2,128)(2,1)} %all_to_all.37) | data formatting | bytes 8388608
  244.2 6.6 %copy.42 = bf16[1,512,4096]{1,2,0:T(8,128)(2,1)} copy(bf16[1,512,4096]{1,0,2:T(2,128)(2,1)} %bitcast.90) | data formatting | bytes 8388608
  250.8 6.3 %copy.33 = bf16[1,4,512,1024]{3,2,1,0:T(8,128)(2,1)} copy(bf16[1,4,512,1024]{2,3,1,0:T(8,128)(2,1)} %bitcast.91) | data formatting | bytes 8388608 | tf_op jit(solution)/shard_map/all_to_all | solution.py:63
  257.1 0.0 all-gather.8.cloned.1.call-update
  257.1 0.0 all-gather.4.cloned.1.call-done
  257.2 1.8 collective-permute-start
  259.0 0.0 copy-done
  259.0 0.6 constant_dynamic-slice_fusion
  259.6 0.6 iota_compare_fusion.1
  260.2 0.6 fusion.43
  260.9 0.1 fusion.40
  261.0 0.0 all-gather.6.cloned.1.call-done
  261.0 178.3 %collective-permute-done = bf16[1,1,512,8192]{3,2,1,0:T(8,128)(2,1)} collective-permute-done((bf16[1,1,512,8192]{3,2,1,0:T(8,128)(2,1)}, bf16[1,1,512,8192]{3,2,1,0:T(8,128)(2,1)}, u32[]{:S(2)}, u32[]{:S(2)}) %collective-permute-start) | collective-permute-done | bytes 8388640 | tf_op jit(solution)/shard_map/ppermute | solution.py:13
  439.4 6.9 %fusion.32 = bf16[1,512,1,256]{3,1,2,0:T(8,128)(2,1)S(1)} fusion(bf16[1,8192,256]{2,1,0:T(8,128)(2,1)} %all-gather.6.cloned.1.call-done, bf16[1,1,512,8192]{3,2,1,0:T(8,128)(2,1)} %collective-permute-done), kind=kOutput, calls=%fused_computation.24 | convolution fusion | flops 2147614720 | bytes 12845056 | tf_op jit(solution)/shard_map/dot_general | solution.py:73
  446.3 98.3 %all-gather.8.cloned.1.call-done = bf16[1,8192,1024]{2,1,0:T(8,128)(2,1)} async-done(((bf16[1,2048,1024]{2,1,0:T(8,128)(2,1)}), bf16[1,8192,1024]{2,1,0:T(8,128)(2,1)}) %all-gather.8.cloned.1.call-update) | async-done | bytes 16777232 | tf_op jit(solution)/shard_map/all_gather | solution.py:69
  544.6 14.8 %fusion.22 = bf16[64,8,8,128]{3,2,1,0:T(8,128)(2,1)S(1)} fusion(bf16[1,8192,1024]{2,1,0:T(8,128)(2,1)} %all-gather.8.cloned.1.call-done, bf16[1,1,512,8192]{3,2,1,0:T(8,128)(2,1)} %collective-permute-done), kind=kOutput, calls=%fused_computation.22 | convolution fusion | flops 8590458880 | bytes 26214400 | tf_op jit(solution)/shard_map/dot_general | solution.py:72
  559.4 1.6 fusion.6
  561.0 1.8 fusion.5
  562.8 0.0 copy-start.1
  562.8 2.7 fusion.14
  565.4 1.3 copy.37
  566.8 0.0 copy-done.1
  (2 shorter events, 0.0 us)
Async XLA Ops:
  6.5 252.4 %copy-start = (s32[2,1]{0,1:T(1,128)S(1)}, s32[2,1]{0,1:T(1,128)}, u32[]{:S(2)}) copy-start(s32[2,1]{0,1:T(1,128)} %param.6) | copy-start | bytes 28
  6.5 6.6 %copy-start.2 = (bf16[1,512,1024]{2,1,0:T(8,128)(2,1)S(1)}, bf16[1,512,1024]{2,1,0:T(8,128)(2,1)}, u32[]{:S(2)}) copy-start(bf16[1,512,1024]{2,1,0:T(8,128)(2,1)} %param.9) | copy-start | bytes 3145732
  6.5 250.6 %all-gather.4.cloned.1.call-start = ((), (), s32[]{:S(2)}) async-start(), calls=%async_computation.2 | async-start | bytes 10485760 | tf_op jit(solution)/shard_map/all_gather | solution.py:56
  13.1 247.9 %all-gather.6.cloned.1.call-start = ((), (), s32[]{:S(2)}) async-start(), calls=%async_computation.3 | async-start | bytes 5242880 | tf_op jit(solution)/shard_map/all_gather | solution.py:70
  13.2 27.0 %collective-permute-start.1 = (bf16[1,512,1024]{2,1,0:T(8,128)(2,1)S(1)}, bf16[1,512,1024]{2,1,0:T(8,128)(2,1)S(1)}, u32[]{:S(2)}, u32[]{:S(2)}) collective-permute-start(bf16[1,512,1024]{2,1,0:T(8,128)(2,1)S(1)} %copy-done.2), channel_id=1, source_target_pairs={{0,16},{16,0},{1,17},{17,1},{2,18},{18,2},{3,19},{19,3},{4,20},{20... | collective-permute-start | bytes 3145736 | tf_op jit(solution)/shard_map/ppermute | solution.py:13
  16.2 113.1 %collective-permute-start.2 = (bf16[1,512,4096]{2,1,0:T(8,128)(2,1)}, bf16[1,512,4096]{2,1,0:T(8,128)(2,1)}, u32[]{:S(2)}, u32[]{:S(2)}) collective-permute-start(bf16[1,512,4096]{2,1,0:T(8,128)(2,1)} %param.8), channel_id=1, source_target_pairs={{0,16},{16,0},{1,17},{17,1},{2,18},{18,2},{3,19},{19,3},{4,20},{20... | collective-permute-start | bytes 12582920 | tf_op jit(solution)/shard_map/ppermute | solution.py:13
  82.5 462.1 %all-gather.8.cloned.1.call-start = ((), (), s32[]{:S(2)}) async-start(), calls=%async_computation.4 | async-start | bytes 20971520 | tf_op jit(solution)/shard_map/all_gather | solution.py:69
  257.2 182.2 %collective-permute-start = (bf16[1,1,512,8192]{3,2,1,0:T(8,128)(2,1)}, bf16[1,1,512,8192]{3,2,1,0:T(8,128)(2,1)}, u32[]{:S(2)}, u32[]{:S(2)}) collective-permute-start(bf16[1,1,512,8192]{3,2,1,0:T(8,128)(2,1)} %all-gather.4.cloned.1.call-done), channel_id=1, source_target_pairs={{0,16},{16,0},{1,17},{17,1},{2,18},{18,2},{3,19},{19,3},{4,20},{20... | collective-permute-start | bytes 25165832 | tf_op jit(solution)/shard_map/ppermute | solution.py:13
  562.8 4.0 copy-start.1
Sparse Core Ops, SparseCore 0:
  13.2 72.2 all-gather.3
  87.0 80.7 all-gather.5
  257.3 287.2 all-gather.7
where the time goes:
time: 575 us; the launch traced here: 573 us
  waiting for transfers between devices  347 us (60%)
  blocking collectives  83 us (14%)
  local copies, waits for them, and re-layouts  53.2 us (9%)
  other arithmetic  45.4 us (8%)
  matrix products  26 us (5%)
  between operations  13.2 us (2%)
    ppermute x3, waiting for transfers between devices, partner(): lax.ppermute(value, axis, [(i, i ^ 1 << distance) for i in range(lax.axis...  249 us
    all_gather x1, waiting for transfers between devices, on_device(): lax.all_gather(query_cols, 'dp', axis=1, tiled=True)  98.3 us
    all_to_all x1, blocking collectives, on_device(): lax.all_to_all(rows_query, 'mp', split_axis=2, concat_axis=1, tiled=True)  53.8 us
    unnamed x2, other arithmetic  35.7 us
    all_to_all x1, blocking collectives, on_device(): lax.all_to_all(rows_keyval, 'mp', split_axis=2, concat_axis=1, tiled=True)  29.2 us
    unnamed x13, local copies, waits for them, and re-layouts  22.9 us
    ppermute x2, local copies, waits for them, and re-layouts, partner(): lax.ppermute(value, axis, [(i, i ^ 1 << distance) for i in range(lax.axis...  20.7 us
    dot_general x1, matrix products, on_device(): query = jnp.dot(tokens, full_query[0], preferred_element_type=jnp.float32)  14.8 us
  transfers between devices with their start and end apart: 6, of which 4 were waited for; matrix products, arithmetic and copies ran while one was open for 17% of the time, Pallas kernels for 0%

commit v1 on v0

--- a/solution.py
+++ b/solution.py
@@ -60,7 +60,12 @@
     tokens = whole[0].reshape(rollouts * seqlen, whole.shape[3])
     rows_query, rows_keyval = partner((w_query, w_keyval), "pool", 0)
     query_cols, keyval_cols = (
-        lax.all_to_all(rows_query, "mp", split_axis=2, concat_axis=1, tiled=True),
+        jnp.concatenate(
+            lax.all_to_all(
+                jnp.stack(jnp.split(rows_query, lax.axis_size("mp"), axis=2)), "mp", 0, 0
+            ),
+            axis=1,
+        ),
         lax.all_to_all(rows_keyval, "mp", split_axis=2, concat_axis=1, tiled=True),
     )
     width_query = query_cols.shape[2]

time: 575 us -> 501 us (0.87)
  local copies, waits for them, and re-layouts: 53.2 us -> 10.3 us
  other arithmetic: 45.4 us -> 17.5 us
    unnamed x2 -> x1, other arithmetic: 35.7 us -> 7.31 us
    unnamed x13 -> x10, local copies, waits for them, and re-layouts: 22.9 us -> 2.56 us
    ppermute x2 -> x1, local copies, waits for them, and re-layouts: 20.7 us -> 1.82 us  [partner(): lax.ppermute(value, axis, [(i, i ^ 1 << distance) for i in range(lax.axis...]
    all_to_all x1 -> x0, local copies, waits for them, and re-layouts: 6.34 us -> none  [on_device(): lax.all_to_all(rows_query, 'mp', split_axis=2, concat_axis=1, tiled=True)]
  transfers between devices with their start and end apart: 6 -> 6, of which waited for: 4 -> 4; matrix products, arithmetic and copies ran while one was open for 17% -> 5% of each run, Pallas kernels for 0% -> 0%
where the time goes in v1:
time: 501 us; the launch traced here: 500 us
  waiting for transfers between devices  347 us (69%)
  blocking collectives  80.8 us (16%)
  matrix products  26 us (5%)
  other arithmetic  17.5 us (3%)
  between operations  13.2 us (3%)
  local copies, waits for them, and re-layouts  10.3 us (2%)
    ppermute x3, waiting for transfers between devices, partner(): lax.ppermute(value, axis, [(i, i ^ 1 << distance) for i in range(lax.axis...  249 us
    all_gather x1, waiting for transfers between devices, on_device(): lax.all_gather(query_cols, 'dp', axis=1, tiled=True)  98.2 us
    all_to_all x1, blocking collectives, on_device(): lax.all_to_all(jnp.stack(jnp.split(rows_query, lax.axis_size('mp'), axis=...  51.5 us
    all_to_all x1, blocking collectives, on_device(): lax.all_to_all(rows_keyval, 'mp', split_axis=2, concat_axis=1, tiled=True)  29.2 us
    dot_general x1, matrix products, on_device(): query = jnp.dot(tokens, full_query[0], preferred_element_type=jnp.float32)  14.8 us
  transfers between devices with their start and end apart: 6, of which 4 were waited for; matrix products, arithmetic and copies ran while one was open for 5% of the time, Pallas kernels for 0%

profile of v1, /device:TPU:0, one launch (start us, length us, event | category | flops | bytes accessed | tf_op | source)
XLA Modules:
  0.0 500.2 jit_solution(4993964522386417077)
XLA Ops:
  6.5 0.0 copy-start
  6.5 0.0 all-gather.4.cloned.1.call-start
  6.5 0.0 copy-start.2
  6.5 2.2 fusion.7
  8.7 0.8 dynamic-slice_convert_fusion
  9.5 3.5 fusion.9
  13.0 0.0 all-gather.4.cloned.1.call-update
  13.1 0.0 all-gather.6.cloned.1.call-start
  13.1 0.0 copy-done.2
  13.1 3.0 collective-permute-start.1
  16.1 0.1 collective-permute-start.2
  16.2 23.9 %collective-permute-done.1 = bf16[1,512,1024]{2,1,0:T(8,128)(2,1)S(1)} collective-permute-done((bf16[1,512,1024]{2,1,0:T(8,128)(2,1)S(1)}, bf16[1,512,1024]{2,1,0:T(8,128)(2,1)S(1)}, u32[]{:S(2)}, u32[]{:S(2)}) %collective-permute-start.1) | collective-permute-done | bytes 1048608 | tf_op jit(solution)/shard_map/ppermute | solution.py:13
  40.2 1.8 copy.26
  42.0 0.5 broadcast.68
  42.5 7.3 %reduce.3 = bf16[1024,512]{1,0:T(8,128)(2,1)S(1)} reduce(bf16[1024,1,512]{2,1,0:T(2,128)(2,1)S(1)} %bitcast.94, bf16[]{:T(256)} %broadcast.68), dimensions={1}, to_apply=%bitcast.86.reduce_sub_computation | reduce | bytes 2097154
  49.8 0.8 reshape.126
  50.6 29.2 %all_to_all.23 = bf16[4,2,65536]{2,1,0:T(2,128)(2,1)S(1)} all-to-all(bf16[4,2,65536]{2,1,0:T(2,128)(2,1)S(1)} %reshape.126), channel_id=1, replica_groups=mesh['pool'=2,'dp'=4,'mp'=4] {'mp'}, dimensions={0} | all-to-all | bytes 2097152 | tf_op jit(solution)/shard_map/all_to_all | solution.py:69
  79.8 1.0 reshape.127
  80.8 0.3 copy.35
  81.1 1.3 copy.27
  82.4 0.0 all-gather.6.cloned.1.call-update
  82.4 0.0 all-gather.8.cloned.1.call-start
  82.5 46.8 %collective-permute-done.2 = bf16[1,512,4096]{2,1,0:T(8,128)(2,1)} collective-permute-done((bf16[1,512,4096]{2,1,0:T(8,128)(2,1)}, bf16[1,512,4096]{2,1,0:T(8,128)(2,1)}, u32[]{:S(2)}, u32[]{:S(2)}) %collective-permute-start.2) | collective-permute-done | bytes 4194336 | tf_op jit(solution)/shard_map/ppermute | solution.py:13
  129.3 2.7 slice_bitcast_fusion.3
  132.0 0.6 pad_maximum_fusion
  132.6 51.5 %all_to_all.24 = bf16[4,1,512,1024]{3,2,1,0:T(8,128)(2,1)} all-to-all(bf16[4,1,512,1024]{3,2,1,0:T(8,128)(2,1)S(1)} %pad_maximum_fusion), channel_id=1, replica_groups=mesh['pool'=2,'dp'=4,'mp'=4] {'mp'}, dimensions={0} | all-to-all | bytes 8388608 | tf_op jit(solution)/shard_map/all_to_all | solution.py:64
  184.1 0.0 all-gather.8.cloned.1.call-update
  184.1 0.0 all-gather.4.cloned.1.call-done
  184.2 1.8 collective-permute-start
  186.0 0.0 copy-done
  186.0 0.6 constant_dynamic-slice_fusion
  186.6 0.6 iota_compare_fusion.1
  187.2 0.6 fusion.43
  187.9 0.1 fusion.40
  188.0 0.0 all-gather.6.cloned.1.call-done
  188.0 178.3 %collective-permute-done = bf16[1,1,512,8192]{3,2,1,0:T(8,128)(2,1)} collective-permute-done((bf16[1,1,512,8192]{3,2,1,0:T(8,128)(2,1)}, bf16[1,1,512,8192]{3,2,1,0:T(8,128)(2,1)}, u32[]{:S(2)}, u32[]{:S(2)}) %collective-permute-start) | collective-permute-done | bytes 8388640 | tf_op jit(solution)/shard_map/ppermute | solution.py:13
  366.4 6.9 %fusion.32 = bf16[1,512,1,256]{3,1,2,0:T(8,128)(2,1)S(1)} fusion(bf16[1,8192,256]{2,1,0:T(8,128)(2,1)} %all-gather.6.cloned.1.call-done, bf16[1,1,512,8192]{3,2,1,0:T(8,128)(2,1)} %collective-permute-done), kind=kOutput, calls=%fused_computation.25 | convolution fusion | flops 2147614720 | bytes 12845056 | tf_op jit(solution)/shard_map/dot_general | solution.py:78
  373.3 98.2 %all-gather.8.cloned.1.call-done = bf16[1,8192,1024]{2,1,0:T(8,128)(2,1)} async-done(((bf16[1,2048,1024]{2,1,0:T(8,128)(2,1)}), bf16[1,8192,1024]{2,1,0:T(8,128)(2,1)}) %all-gather.8.cloned.1.call-update) | async-done | bytes 16777232 | tf_op jit(solution)/shard_map/all_gather | solution.py:74
  471.5 14.8 %fusion.22 = bf16[64,8,8,128]{3,2,1,0:T(8,128)(2,1)S(1)} fusion(bf16[1,8192,1024]{2,1,0:T(8,128)(2,1)} %all-gather.8.cloned.1.call-done, bf16[1,1,512,8192]{3,2,1,0:T(8,128)(2,1)} %collective-permute-done), kind=kOutput, calls=%fused_computation.23 | convolution fusion | flops 8590458880 | bytes 26214400 | tf_op jit(solution)/shard_map/dot_general | solution.py:77
  486.3 1.6 fusion.6
  488.0 1.7 fusion.5
  489.7 0.0 copy-start.1
  489.7 2.7 fusion.14
  492.4 1.3 copy.31
  493.7 0.0 copy-done.1
  (1 shorter events, 0.0 us)
Async XLA Ops:
  6.5 179.4 %copy-start = (s32[2,1]{0,1:T(1,128)S(1)}, s32[2,1]{0,1:T(1,128)}, u32[]{:S(2)}) copy-start(s32[2,1]{0,1:T(1,128)} %param.6) | copy-start | bytes 28
  6.5 177.6 %all-gather.4.cloned.1.call-start = ((), (), s32[]{:S(2)}) async-start(), calls=%async_computation.2 | async-start | bytes 10485760 | tf_op jit(solution)/shard_map/all_gather | solution.py:56
  6.5 6.6 %copy-start.2 = (bf16[1,512,1024]{2,1,0:T(8,128)(2,1)S(1)}, bf16[1,512,1024]{2,1,0:T(8,128)(2,1)}, u32[]{:S(2)}) copy-start(bf16[1,512,1024]{2,1,0:T(8,128)(2,1)} %param.9) | copy-start | bytes 3145732
  13.1 175.0 %all-gather.6.cloned.1.call-start = ((), (), s32[]{:S(2)}) async-start(), calls=%async_computation.3 | async-start | bytes 5242880 | tf_op jit(solution)/shard_map/all_gather | solution.py:75
  13.1 27.0 %collective-permute-start.1 = (bf16[1,512,1024]{2,1,0:T(8,128)(2,1)S(1)}, bf16[1,512,1024]{2,1,0:T(8,128)(2,1)S(1)}, u32[]{:S(2)}, u32[]{:S(2)}) collective-permute-start(bf16[1,512,1024]{2,1,0:T(8,128)(2,1)S(1)} %copy-done.2), channel_id=1, source_target_pairs={{0,16},{16,0},{1,17},{17,1},{2,18},{18,2},{3,19},{19,3},{4,20},{20... | collective-permute-start | bytes 3145736 | tf_op jit(solution)/shard_map/ppermute | solution.py:13
  16.1 113.1 %collective-permute-start.2 = (bf16[1,512,4096]{2,1,0:T(8,128)(2,1)}, bf16[1,512,4096]{2,1,0:T(8,128)(2,1)}, u32[]{:S(2)}, u32[]{:S(2)}) collective-permute-start(bf16[1,512,4096]{2,1,0:T(8,128)(2,1)} %param.8), channel_id=1, source_target_pairs={{0,16},{16,0},{1,17},{17,1},{2,18},{18,2},{3,19},{19,3},{4,20},{20... | collective-permute-start | bytes 12582920 | tf_op jit(solution)/shard_map/ppermute | solution.py:13
  82.4 389.1 %all-gather.8.cloned.1.call-start = ((), (), s32[]{:S(2)}) async-start(), calls=%async_computation.4 | async-start | bytes 20971520 | tf_op jit(solution)/shard_map/all_gather | solution.py:74
  184.2 182.2 %collective-permute-start = (bf16[1,1,512,8192]{3,2,1,0:T(8,128)(2,1)}, bf16[1,1,512,8192]{3,2,1,0:T(8,128)(2,1)}, u32[]{:S(2)}, u32[]{:S(2)}) collective-permute-start(bf16[1,1,512,8192]{3,2,1,0:T(8,128)(2,1)} %all-gather.4.cloned.1.call-done), channel_id=1, source_target_pairs={{0,16},{16,0},{1,17},{17,1},{2,18},{18,2},{3,19},{19,3},{4,20},{20... | collective-permute-start | bytes 25165832 | tf_op jit(solution)/shard_map/ppermute | solution.py:13
  489.7 4.0 copy-start.1
Sparse Core Ops, SparseCore 0:
  13.2 72.2 all-gather.3
  87.0 80.7 all-gather.5
  184.3 287.2 all-gather.7
